TPU v7x, 32 devices: a whole 2x2x4 slice. The times are simulated.
32 devices in a mesh: srow: 4 (over y, core), scol: 8 (over z, x).
Axes of the slice: x: 2, y: 2, z: 4, core: 2. Of those that a mesh axis runs over, the one named last changes fastest.
Arguments:
- loads: float32 [4, 16, 4, 128], P('srow', 'scol'), may hold values from -6 to 6
- local_inverse: float32 [4, 16, 128, 128], P('srow', 'scol'), as said below
- dirichlet: float32 [4, 16, 128, 128], P('srow', 'scol'), as said below
- corner_coupling: float32 [4, 16, 128], P('srow', 'scol'), may hold values from -4 to 4
- coarse_inverse: float32 [4, 16, 16], P('srow', 'scol'), as said below
- partner: int32 [4, 16, 128], P('srow', 'scol'), may hold values from -1 to 31, as said below
Outputs:
- multipliers: float32 [4, 16, 4, 128], P('srow', 'scol')
- residual: float32 [4, 16, 4, 128], P('srow', 'scol')
Inputs may be any that keep to these rules, and one draw needn't show every extreme that they name: `partner`: on each edge of each subdomain the first n entries, for some n of 1 to 32, are the positions 0 to n - 1 in order or reversed, the rest are -1; the two subdomains sharing an edge have the same n and mutually inverse lists. `local_inverse`: each block is symmetric positive definite. `dirichlet`: each block is symmetric positive definite. `coarse_inverse`: each band's matrix is symmetric positive definite.
All inputs are finite; a program needn't handle non-finite values.
Results may differ from a plain program's by a relative error of at most 0.0003.
Values sent between devices are 32-bit elements; how exact they have to be, the bound alone decides.
A program may use at most 64 MiB of HBM per device.

v0:
```python
import jax
import jax.numpy as jnp
from jax import lax
from jax.sharding import PartitionSpec as P

ITERS = 3
precise = lax.Precision.HIGHEST


def with_halo(cells, sides, width):
    for axis, dim in sides:
        count = lax.axis_size(axis)
        head = lax.slice_in_dim(cells, 0, width, axis=dim)
        tail = lax.slice_in_dim(cells, cells.shape[dim] - width, cells.shape[dim], axis=dim)
        cells = jnp.concatenate(
            [
                lax.ppermute(tail, axis, [(i, (i + 1) % count) for i in range(count)]),
                cells,
                lax.ppermute(head, axis, [((i + 1) % count, i) for i in range(count)]),
            ],
            axis=dim,
        )
    return cells


def facing_edges(values):
    edge_len = values.shape[-1] // 4
    sideways = with_halo(values[..., 0 : 2 * edge_len], (("scol", 1),), 1)
    vertical = with_halo(values[..., 2 * edge_len :], (("srow", 0),), 1)
    west_side = sideways[:, :-2, :, edge_len : 2 * edge_len]
    east_side = sideways[:, 2:, :, 0:edge_len]
    south_side = vertical[:-2, :, :, edge_len : 2 * edge_len]
    north_side = vertical[2:, :, :, 0:edge_len]
    return jnp.concatenate([west_side, east_side, south_side, north_side], axis=-1)


def jump(values, partner):
    edge_len = values.shape[-1] // 4
    facing = facing_edges(values)
    offset = jnp.arange(values.shape[-1], dtype=jnp.int32) // edge_len * edge_len
    position = jnp.clip(partner, 0, edge_len - 1) + offset
    position = jnp.broadcast_to(position[:, :, None, :], values.shape)
    picked = jnp.take_along_axis(facing, position, axis=-1)
    return jnp.where(partner[:, :, None, :] >= 0, values - picked, jnp.zeros_like(values))


def apply_inverse(values, local_inverse, corner_coupling, coarse_inverse):
    sub_rows, sub_cols, rhs_count, width = values.shape
    blocks = jnp.einsum("ijab,ijrb->ijra", local_inverse, values, precision=precise)
    coarse_in = jnp.einsum("ijb,ijrb->ijr", corner_coupling, values, precision=precise)
    coarse_in = coarse_in.reshape(sub_rows * sub_cols, rhs_count)
    band_rows = coarse_inverse[0]
    coarse_out = jnp.dot(
        band_rows,
        lax.all_gather(coarse_in, "scol", axis=0, tiled=True),
        precision=precise,
        preferred_element_type=jnp.float32,
    )
    coarse_out = coarse_out.reshape(sub_rows, sub_cols, rhs_count)
    return blocks + corner_coupling[:, :, None, :] * coarse_out[..., None]


def inner(left, right):
    return jnp.sum(left * right, axis=(0, 1, 3))


def global_sums(first_dot, second_dot):
    return lax.psum((first_dot, second_dot), ("srow", "scol"))


def scaled(coef, values):
    return coef[None, None, :, None] * values


def body(loads, local_inverse, dirichlet, corner_coupling, coarse_inverse, partner):

    def operator(values):
        spread = jump(values, partner)
        return jump(apply_inverse(spread, local_inverse, corner_coupling, coarse_inverse), partner)

    def precond(values):
        spread = jump(values, partner)
        return jump(jnp.einsum("ijab,ijrb->ijra", dirichlet, spread, precision=precise), partner)

    right = operator(loads)
    multipliers = jnp.zeros_like(right)
    residual = right
    precon = precond(residual)
    image = operator(precon)
    gamma, curvature = global_sums(inner(residual, precon), inner(precon, image))
    step_size = gamma / curvature
    search = precon
    along = image
    for iteration in range(ITERS):
        multipliers = multipliers + scaled(step_size, search)
        residual = residual - scaled(step_size, along)
        if iteration + 1 < ITERS:
            precon = precond(residual)
            image = operator(precon)
            gamma_new, curvature = global_sums(inner(residual, precon), inner(precon, image))
            dir_ratio = gamma_new / gamma
            step_size = gamma_new / (curvature - dir_ratio * gamma_new / step_size)
            search = precon + scaled(dir_ratio, search)
            along = image + scaled(dir_ratio, along)
            gamma = gamma_new
    return (multipliers, residual)


def solution(mesh):
    return jax.shard_map(
        body,
        mesh=mesh,
        in_specs=(
            P("srow", "scol", None, None),
            P("srow", "scol", None, None),
            P("srow", "scol", None, None),
            P("srow", "scol", None),
            P("srow", "scol", None),
            P("srow", "scol", None),
        ),
        out_specs=(P("srow", "scol", None, None), P("srow", "scol", None, None)),
        check_vma=False,
    )
```

profile of v0, /device:TPU:0, one launch (start us, length us, event | category | flops | bytes accessed | tf_op | source)
XLA Modules:
  0.0 464.1 jit_solution(16173901481340105120)
XLA Ops:
  2.0 1.9 collective-permute-start.3
  4.0 2.3 collective-permute-start
  6.2 3.1 collective-permute-start.1
  10.9 9.6 %gather_fusion = f32[1024]{0:T(1024)S(1)} fusion(f32[2,4,128]{2,1,0:T(4,128)S(1)} %fusion.69, s32[1024]{0:T(1024)S(1)} %bitcast.196), kind=kCustom, calls=%fused_computation.clone | custom fusion | bytes 20480 | tf_op jit(solution)/shard_map/jit(take_along_axis)/gather | solution.py:43
  21.3 21.1 %all-gather = f32[8,2,4]{2,1,0:T(2,128)S(1)} all-gather(f32[1,2,4]{2,1,0:T(2,128)S(1)} %bitcast.256), channel_id=1, replica_groups=mesh['srow'=4,'scol'=8] {'scol'}, dimensions={0}, use_global_device_ids=true | all-gather | bytes 288 | tf_op jit(solution)/shard_map/all_gather | solution.py:55
  43.6 1.7 collective-permute-start.7
  45.4 4.7 %collective-permute-start.5 = (f32[1,1,4,64]{3,2,1,0:T(4,128)S(1)}, f32[1,1,4,64]{3,2,1,0:T(4,128)S(1)}, u32[]{:S(2)}, u32[]{:S(2)}) collective-permute-start(f32[1,1,4,64]{3,2,1,0:T(4,128)S(1)} %get-tuple-element.76), channel_id=1, source_target_pairs={{1,0},{2,1},{3,2},{4,3},{5,4},{6,5},{7,6},{0,7},{9,8},{10,9},{11,1... | collective-permute-start | bytes 3080 | tf_op jit(solution)/shard_map/ppermute | solution.py:19
  51.7 9.6 %gather_fusion.1 = f32[1024]{0:T(1024)S(1)} fusion(f32[2,4,128]{2,1,0:T(4,128)S(1)} %fusion.65, s32[1024]{0:T(1024)S(1)} %bitcast.197), kind=kCustom, calls=%fused_computation.1.clone | custom fusion | bytes 20480 | tf_op jit(solution)/shard_map/jit(take_along_axis)/gather | solution.py:43
  63.2 4.7 %collective-permute-start.9 = (f32[1,1,4,64]{3,2,1,0:T(4,128)S(1)}, f32[1,1,4,64]{3,2,1,0:T(4,128)S(1)}, u32[]{:S(2)}, u32[]{:S(2)}) collective-permute-start(f32[1,1,4,64]{3,2,1,0:T(4,128)S(1)} %get-tuple-element.72), channel_id=1, source_target_pairs={{1,0},{2,1},{3,2},{4,3},{5,4},{6,5},{7,6},{0,7},{9,8},{10,9},{11,1... | collective-permute-start | bytes 3080 | tf_op jit(solution)/shard_map/ppermute | solution.py:19
  69.6 9.6 %gather_fusion.2 = f32[1024]{0:T(1024)S(1)} fusion(f32[2,4,128]{2,1,0:T(4,128)S(1)} %fusion.61, s32[1024]{0:T(1024)S(1)} %bitcast.198), kind=kCustom, calls=%fused_computation.2.clone | custom fusion | bytes 20480 | tf_op jit(solution)/shard_map/jit(take_along_axis)/gather | solution.py:43
  79.6 1.8 collective-permute-start.15
  81.3 4.7 %collective-permute-start.13 = (f32[1,1,4,64]{3,2,1,0:T(4,128)S(1)}, f32[1,1,4,64]{3,2,1,0:T(4,128)S(1)}, u32[]{:S(2)}, u32[]{:S(2)}) collective-permute-start(f32[1,1,4,64]{3,2,1,0:T(4,128)S(1)} %get-tuple-element.68), channel_id=1, source_target_pairs={{1,0},{2,1},{3,2},{4,3},{5,4},{6,5},{7,6},{0,7},{9,8},{10,9},{11,1... | collective-permute-start | bytes 3080 | tf_op jit(solution)/shard_map/ppermute | solution.py:19
  87.7 9.6 %gather_fusion.3 = f32[1024]{0:T(1024)S(1)} fusion(f32[2,4,128]{2,1,0:T(4,128)S(1)} %fusion.57, s32[1024]{0:T(1024)S(1)} %bitcast.199), kind=kCustom, calls=%fused_computation.3.clone | custom fusion | bytes 20480 | tf_op jit(solution)/shard_map/jit(take_along_axis)/gather | solution.py:43
  99.2 4.7 %collective-permute-start.17 = (f32[1,1,4,64]{3,2,1,0:T(4,128)S(1)}, f32[1,1,4,64]{3,2,1,0:T(4,128)S(1)}, u32[]{:S(2)}, u32[]{:S(2)}) collective-permute-start(f32[1,1,4,64]{3,2,1,0:T(4,128)S(1)} %get-tuple-element.64), channel_id=1, source_target_pairs={{1,0},{2,1},{3,2},{4,3},{5,4},{6,5},{7,6},{0,7},{9,8},{10,9},{11,1... | collective-permute-start | bytes 3080 | tf_op jit(solution)/shard_map/ppermute | solution.py:19
  105.5 9.6 %gather_fusion.4 = f32[1024]{0:T(1024)S(1)} fusion(f32[2,4,128]{2,1,0:T(4,128)S(1)} %fusion.53, s32[1024]{0:T(1024)S(1)} %bitcast.200), kind=kCustom, calls=%fused_computation.4.clone | custom fusion | bytes 20480 | tf_op jit(solution)/shard_map/jit(take_along_axis)/gather | solution.py:43
  115.3 21.0 %all-gather.1 = f32[8,2,4]{2,1,0:T(2,128)S(1)} all-gather(f32[1,2,4]{2,1,0:T(2,128)S(1)} %bitcast.257), channel_id=1, replica_groups=mesh['srow'=4,'scol'=8] {'scol'}, dimensions={0}, use_global_device_ids=true | all-gather | bytes 288 | tf_op jit(solution)/shard_map/all_gather | solution.py:55
  136.8 1.7 collective-permute-start.23
  138.6 4.7 %collective-permute-start.21 = (f32[1,1,4,64]{3,2,1,0:T(4,128)S(1)}, f32[1,1,4,64]{3,2,1,0:T(4,128)S(1)}, u32[]{:S(2)}, u32[]{:S(2)}) collective-permute-start(f32[1,1,4,64]{3,2,1,0:T(4,128)S(1)} %get-tuple-element.60), channel_id=1, source_target_pairs={{1,0},{2,1},{3,2},{4,3},{5,4},{6,5},{7,6},{0,7},{9,8},{10,9},{11,1... | collective-permute-start | bytes 3080 | tf_op jit(solution)/shard_map/ppermute | solution.py:19
  144.9 9.6 %gather_fusion.5 = f32[1024]{0:T(1024)S(1)} fusion(f32[2,4,128]{2,1,0:T(4,128)S(1)} %fusion.49, s32[1024]{0:T(1024)S(1)} %bitcast.201), kind=kCustom, calls=%fused_computation.5.clone | custom fusion | bytes 20480 | tf_op jit(solution)/shard_map/jit(take_along_axis)/gather | solution.py:43
  154.7 40.2 %all-reduce.2 = (f32[4]{0:T(128)S(1)}, f32[4]{0:T(128)S(1)}) all-reduce(f32[4]{0:T(128)S(1)} %get-tuple-element.8, f32[4]{0:T(128)S(1)} %get-tuple-element.7), channel_id=1, replica_groups=mesh['srow'=4,'scol'=8] {'srow','scol'}, use_global_device_ids=true, to_apply=%region_1.3 | all-reduce | flops 8 | bytes 64 | tf_op jit(solution)/shard_map/psum | solution.py:68
  195.1 1.7 collective-permute-start.27
  196.8 2.3 collective-permute-start.24
  199.1 2.4 collective-permute-start.25
  203.2 9.6 %gather_fusion.6 = f32[1024]{0:T(1024)S(1)} fusion(f32[2,4,128]{2,1,0:T(4,128)S(1)} %fusion.45, s32[1024]{0:T(1024)S(1)} %bitcast.202), kind=kCustom, calls=%fused_computation.6.clone | custom fusion | bytes 20480 | tf_op jit(solution)/shard_map/jit(take_along_axis)/gather | solution.py:43
  213.2 1.8 collective-permute-start.31
  214.9 1.8 collective-permute-start.28
  216.7 2.9 collective-permute-start.29
  221.3 9.6 %gather_fusion.7 = f32[1024]{0:T(1024)S(1)} fusion(f32[2,4,128]{2,1,0:T(4,128)S(1)} %fusion.41, s32[1024]{0:T(1024)S(1)} %bitcast.203), kind=kCustom, calls=%fused_computation.7.clone | custom fusion | bytes 20480 | tf_op jit(solution)/shard_map/jit(take_along_axis)/gather | solution.py:43
  234.1 3.4 collective-permute-start.33
  239.1 9.6 %gather_fusion.8 = f32[1024]{0:T(1024)S(1)} fusion(f32[2,4,128]{2,1,0:T(4,128)S(1)} %fusion.37, s32[1024]{0:T(1024)S(1)} %bitcast.204), kind=kCustom, calls=%fused_computation.8.clone | custom fusion | bytes 20480 | tf_op jit(solution)/shard_map/jit(take_along_axis)/gather | solution.py:43
  248.9 21.0 %all-gather.2 = f32[8,2,4]{2,1,0:T(2,128)S(1)} all-gather(f32[1,2,4]{2,1,0:T(2,128)S(1)} %bitcast.258), channel_id=1, replica_groups=mesh['srow'=4,'scol'=8] {'scol'}, dimensions={0}, use_global_device_ids=true | all-gather | bytes 288 | tf_op jit(solution)/shard_map/all_gather | solution.py:55
  272.2 4.7 %collective-permute-start.37 = (f32[1,1,4,64]{3,2,1,0:T(4,128)S(1)}, f32[1,1,4,64]{3,2,1,0:T(4,128)S(1)}, u32[]{:S(2)}, u32[]{:S(2)}) collective-permute-start(f32[1,1,4,64]{3,2,1,0:T(4,128)S(1)} %get-tuple-element.44), channel_id=1, source_target_pairs={{1,0},{2,1},{3,2},{4,3},{5,4},{6,5},{7,6},{0,7},{9,8},{10,9},{11,1... | collective-permute-start | bytes 3080 | tf_op jit(solution)/shard_map/ppermute | solution.py:19
  278.5 9.6 %gather_fusion.9 = f32[1024]{0:T(1024)S(1)} fusion(f32[2,4,128]{2,1,0:T(4,128)S(1)} %fusion.33, s32[1024]{0:T(1024)S(1)} %bitcast.205), kind=kCustom, calls=%fused_computation.9.clone | custom fusion | bytes 20480 | tf_op jit(solution)/shard_map/jit(take_along_axis)/gather | solution.py:43
  288.3 40.8 %all-reduce.1 = (f32[4]{0:T(128)S(1)}, f32[4]{0:T(128)S(1)}) all-reduce(f32[4]{0:T(128)S(1)} %get-tuple-element.6, f32[4]{0:T(128)S(1)} %get-tuple-element.5), channel_id=1, replica_groups=mesh['srow'=4,'scol'=8] {'srow','scol'}, use_global_device_ids=true, to_apply=%region_5.7 | all-reduce | flops 8 | bytes 64 | tf_op jit(solution)/shard_map/psum | solution.py:68
  329.3 1.8 collective-permute-start.43
  331.1 2.3 collective-permute-start.40
  333.3 2.4 collective-permute-start.41
  337.4 9.6 %gather_fusion.10 = f32[1024]{0:T(1024)S(1)} fusion(f32[2,4,128]{2,1,0:T(4,128)S(1)} %fusion.29, s32[1024]{0:T(1024)S(1)} %bitcast.206), kind=kCustom, calls=%fused_computation.10.clone | custom fusion | bytes 20480 | tf_op jit(solution)/shard_map/jit(take_along_axis)/gather | solution.py:43
  347.4 1.8 collective-permute-start.47
  349.2 1.8 collective-permute-start.44
  351.0 2.9 collective-permute-start.45
  355.5 9.6 %gather_fusion.11 = f32[1024]{0:T(1024)S(1)} fusion(f32[2,4,128]{2,1,0:T(4,128)S(1)} %fusion.25, s32[1024]{0:T(1024)S(1)} %bitcast.207), kind=kCustom, calls=%fused_computation.11.clone | custom fusion | bytes 20480 | tf_op jit(solution)/shard_map/jit(take_along_axis)/gather | solution.py:43
  368.4 3.4 collective-permute-start.49
  373.4 9.6 %gather_fusion.12 = f32[1024]{0:T(1024)S(1)} fusion(f32[2,4,128]{2,1,0:T(4,128)S(1)} %fusion.21, s32[1024]{0:T(1024)S(1)} %bitcast.208), kind=kCustom, calls=%fused_computation.12.clone | custom fusion | bytes 20480 | tf_op jit(solution)/shard_map/jit(take_along_axis)/gather | solution.py:43
  383.1 21.0 %all-gather.3 = f32[8,2,4]{2,1,0:T(2,128)S(1)} all-gather(f32[1,2,4]{2,1,0:T(2,128)S(1)} %bitcast.259), channel_id=1, replica_groups=mesh['srow'=4,'scol'=8] {'scol'}, dimensions={0}, use_global_device_ids=true | all-gather | bytes 288 | tf_op jit(solution)/shard_map/all_gather | solution.py:55
  406.4 4.7 %collective-permute-start.53 = (f32[1,1,4,64]{3,2,1,0:T(4,128)S(1)}, f32[1,1,4,64]{3,2,1,0:T(4,128)S(1)}, u32[]{:S(2)}, u32[]{:S(2)}) collective-permute-start(f32[1,1,4,64]{3,2,1,0:T(4,128)S(1)} %get-tuple-element.28), channel_id=1, source_target_pairs={{1,0},{2,1},{3,2},{4,3},{5,4},{6,5},{7,6},{0,7},{9,8},{10,9},{11,1... | collective-permute-start | bytes 3080 | tf_op jit(solution)/shard_map/ppermute | solution.py:19
  412.8 9.6 %gather_fusion.13 = f32[1024]{0:T(1024)S(1)} fusion(f32[2,4,128]{2,1,0:T(4,128)S(1)} %fusion.17, s32[1024]{0:T(1024)S(1)} %bitcast.209), kind=kCustom, calls=%fused_computation.13.clone | custom fusion | bytes 20480 | tf_op jit(solution)/shard_map/jit(take_along_axis)/gather | solution.py:43
  422.5 40.8 %all-reduce = (f32[4]{0:T(128)S(1)}, f32[4]{0:T(128)S(1)}) all-reduce(f32[4]{0:T(128)S(1)} %get-tuple-element.4, f32[4]{0:T(128)S(1)} %get-tuple-element.3), channel_id=1, replica_groups=mesh['srow'=4,'scol'=8] {'srow','scol'}, use_global_device_ids=true, to_apply=%region_9.11 | all-reduce | flops 8 | bytes 64 | tf_op jit(solution)/shard_map/psum | solution.py:68
  (187 shorter events, 44.4 us)
Async XLA Ops:
  1.5 7.9 %collective-permute-start.2 = (f32[1,2,4,64]{3,2,1,0:T(4,128)S(1)}, f32[1,2,4,64]{3,2,1,0:T(4,128)S(1)}, u32[]{:S(2)}, u32[]{:S(2)}) collective-permute-start(f32[1,2,4,64]{3,2,1,0:T(4,128)S(1)} %get-tuple-element.77), channel_id=1, source_target_pairs={{0,8},{8,16},{16,24},{24,0},{1,9},{9,17},{17,25},{25,1},{2,10},{10... | collective-permute-start | bytes 6152 | tf_op jit(solution)/shard_map/ppermute | solution.py:17
  2.0 8.8 %collective-permute-start.3 = (f32[1,2,4,64]{3,2,1,0:T(4,128)S(1)}, f32[1,2,4,64]{3,2,1,0:T(4,128)S(1)}, u32[]{:S(2)}, u32[]{:S(2)}) collective-permute-start(f32[1,2,4,64]{3,2,1,0:T(4,128)S(1)} %get-tuple-element.77), channel_id=1, source_target_pairs={{8,0},{16,8},{24,16},{0,24},{9,1},{17,9},{25,17},{1,25},{10,2},{18... | collective-permute-start | bytes 6152 | tf_op jit(solution)/shard_map/ppermute | solution.py:19
  4.0 6.9 %collective-permute-start = (f32[1,1,4,64]{3,2,1,0:T(4,128)S(1)}, f32[1,1,4,64]{3,2,1,0:T(4,128)S(1)}, u32[]{:S(2)}, u32[]{:S(2)}) collective-permute-start(f32[1,1,4,64]{3,2,1,0:T(4,128)S(1)} %get-tuple-element.79), channel_id=1, source_target_pairs={{0,1},{1,2},{2,3},{3,4},{4,5},{5,6},{6,7},{7,0},{8,9},{9,10},{10,1... | collective-permute-start | bytes 3080 | tf_op jit(solution)/shard_map/ppermute | solution.py:17
  43.6 6.5 %collective-permute-start.6 = (f32[1,2,4,64]{3,2,1,0:T(4,128)S(1)}, f32[1,2,4,64]{3,2,1,0:T(4,128)S(1)}, u32[]{:S(2)}, u32[]{:S(2)}) collective-permute-start(f32[1,2,4,64]{3,2,1,0:T(4,128)S(1)} %get-tuple-element.73), channel_id=1, source_target_pairs={{0,8},{8,16},{16,24},{24,0},{1,9},{9,17},{17,25},{25,1},{2,10},{10... | collective-permute-start | bytes 6152 | tf_op jit(solution)/shard_map/ppermute | solution.py:17
  43.6 8.0 %collective-permute-start.7 = (f32[1,2,4,64]{3,2,1,0:T(4,128)S(1)}, f32[1,2,4,64]{3,2,1,0:T(4,128)S(1)}, u32[]{:S(2)}, u32[]{:S(2)}) collective-permute-start(f32[1,2,4,64]{3,2,1,0:T(4,128)S(1)} %get-tuple-element.73), channel_id=1, source_target_pairs={{8,0},{16,8},{24,16},{0,24},{9,1},{17,9},{25,17},{1,25},{10,2},{18... | collective-permute-start | bytes 6152 | tf_op jit(solution)/shard_map/ppermute | solution.py:19
  45.4 6.3 %collective-permute-start.4 = (f32[1,1,4,64]{3,2,1,0:T(4,128)S(1)}, f32[1,1,4,64]{3,2,1,0:T(4,128)S(1)}, u32[]{:S(2)}, u32[]{:S(2)}) collective-permute-start(f32[1,1,4,64]{3,2,1,0:T(4,128)S(1)} %get-tuple-element.75), channel_id=1, source_target_pairs={{0,1},{1,2},{2,3},{3,4},{4,5},{5,6},{6,7},{7,0},{8,9},{9,10},{10,1... | collective-permute-start | bytes 3080 | tf_op jit(solution)/shard_map/ppermute | solution.py:17
  45.4 6.3 %collective-permute-start.5 = (f32[1,1,4,64]{3,2,1,0:T(4,128)S(1)}, f32[1,1,4,64]{3,2,1,0:T(4,128)S(1)}, u32[]{:S(2)}, u32[]{:S(2)}) collective-permute-start(f32[1,1,4,64]{3,2,1,0:T(4,128)S(1)} %get-tuple-element.76), channel_id=1, source_target_pairs={{1,0},{2,1},{3,2},{4,3},{5,4},{6,5},{7,6},{0,7},{9,8},{10,9},{11,1... | collective-permute-start | bytes 3080 | tf_op jit(solution)/shard_map/ppermute | solution.py:19
  61.4 6.5 %collective-permute-start.10 = (f32[1,2,4,64]{3,2,1,0:T(4,128)S(1)}, f32[1,2,4,64]{3,2,1,0:T(4,128)S(1)}, u32[]{:S(2)}, u32[]{:S(2)}) collective-permute-start(f32[1,2,4,64]{3,2,1,0:T(4,128)S(1)} %get-tuple-element.69), channel_id=1, source_target_pairs={{0,8},{8,16},{16,24},{24,0},{1,9},{9,17},{17,25},{25,1},{2,10},{10... | collective-permute-start | bytes 6152 | tf_op jit(solution)/shard_map/ppermute | solution.py:17
  61.5 8.0 %collective-permute-start.11 = (f32[1,2,4,64]{3,2,1,0:T(4,128)S(1)}, f32[1,2,4,64]{3,2,1,0:T(4,128)S(1)}, u32[]{:S(2)}, u32[]{:S(2)}) collective-permute-start(f32[1,2,4,64]{3,2,1,0:T(4,128)S(1)} %get-tuple-element.69), channel_id=1, source_target_pairs={{8,0},{16,8},{24,16},{0,24},{9,1},{17,9},{25,17},{1,25},{10,2},{18... | collective-permute-start | bytes 6152 | tf_op jit(solution)/shard_map/ppermute | solution.py:19
  63.2 6.3 %collective-permute-start.8 = (f32[1,1,4,64]{3,2,1,0:T(4,128)S(1)}, f32[1,1,4,64]{3,2,1,0:T(4,128)S(1)}, u32[]{:S(2)}, u32[]{:S(2)}) collective-permute-start(f32[1,1,4,64]{3,2,1,0:T(4,128)S(1)} %get-tuple-element.71), channel_id=1, source_target_pairs={{0,1},{1,2},{2,3},{3,4},{4,5},{5,6},{6,7},{7,0},{8,9},{9,10},{10,1... | collective-permute-start | bytes 3080 | tf_op jit(solution)/shard_map/ppermute | solution.py:17
  63.2 6.3 %collective-permute-start.9 = (f32[1,1,4,64]{3,2,1,0:T(4,128)S(1)}, f32[1,1,4,64]{3,2,1,0:T(4,128)S(1)}, u32[]{:S(2)}, u32[]{:S(2)}) collective-permute-start(f32[1,1,4,64]{3,2,1,0:T(4,128)S(1)} %get-tuple-element.72), channel_id=1, source_target_pairs={{1,0},{2,1},{3,2},{4,3},{5,4},{6,5},{7,6},{0,7},{9,8},{10,9},{11,1... | collective-permute-start | bytes 3080 | tf_op jit(solution)/shard_map/ppermute | solution.py:19
  79.6 6.5 %collective-permute-start.14 = (f32[1,2,4,64]{3,2,1,0:T(4,128)S(1)}, f32[1,2,4,64]{3,2,1,0:T(4,128)S(1)}, u32[]{:S(2)}, u32[]{:S(2)}) collective-permute-start(f32[1,2,4,64]{3,2,1,0:T(4,128)S(1)} %get-tuple-element.65), channel_id=1, source_target_pairs={{0,8},{8,16},{16,24},{24,0},{1,9},{9,17},{17,25},{25,1},{2,10},{10... | collective-permute-start | bytes 6152 | tf_op jit(solution)/shard_map/ppermute | solution.py:17
  79.6 8.0 %collective-permute-start.15 = (f32[1,2,4,64]{3,2,1,0:T(4,128)S(1)}, f32[1,2,4,64]{3,2,1,0:T(4,128)S(1)}, u32[]{:S(2)}, u32[]{:S(2)}) collective-permute-start(f32[1,2,4,64]{3,2,1,0:T(4,128)S(1)} %get-tuple-element.65), channel_id=1, source_target_pairs={{8,0},{16,8},{24,16},{0,24},{9,1},{17,9},{25,17},{1,25},{10,2},{18... | collective-permute-start | bytes 6152 | tf_op jit(solution)/shard_map/ppermute | solution.py:19
  81.3 6.3 %collective-permute-start.12 = (f32[1,1,4,64]{3,2,1,0:T(4,128)S(1)}, f32[1,1,4,64]{3,2,1,0:T(4,128)S(1)}, u32[]{:S(2)}, u32[]{:S(2)}) collective-permute-start(f32[1,1,4,64]{3,2,1,0:T(4,128)S(1)} %get-tuple-element.67), channel_id=1, source_target_pairs={{0,1},{1,2},{2,3},{3,4},{4,5},{5,6},{6,7},{7,0},{8,9},{9,10},{10,1... | collective-permute-start | bytes 3080 | tf_op jit(solution)/shard_map/ppermute | solution.py:17
  81.3 6.3 %collective-permute-start.13 = (f32[1,1,4,64]{3,2,1,0:T(4,128)S(1)}, f32[1,1,4,64]{3,2,1,0:T(4,128)S(1)}, u32[]{:S(2)}, u32[]{:S(2)}) collective-permute-start(f32[1,1,4,64]{3,2,1,0:T(4,128)S(1)} %get-tuple-element.68), channel_id=1, source_target_pairs={{1,0},{2,1},{3,2},{4,3},{5,4},{6,5},{7,6},{0,7},{9,8},{10,9},{11,1... | collective-permute-start | bytes 3080 | tf_op jit(solution)/shard_map/ppermute | solution.py:19
  97.4 6.5 %collective-permute-start.18 = (f32[1,2,4,64]{3,2,1,0:T(4,128)S(1)}, f32[1,2,4,64]{3,2,1,0:T(4,128)S(1)}, u32[]{:S(2)}, u32[]{:S(2)}) collective-permute-start(f32[1,2,4,64]{3,2,1,0:T(4,128)S(1)} %get-tuple-element.61), channel_id=1, source_target_pairs={{0,8},{8,16},{16,24},{24,0},{1,9},{9,17},{17,25},{25,1},{2,10},{10... | collective-permute-start | bytes 6152 | tf_op jit(solution)/shard_map/ppermute | solution.py:17
  97.4 8.0 %collective-permute-start.19 = (f32[1,2,4,64]{3,2,1,0:T(4,128)S(1)}, f32[1,2,4,64]{3,2,1,0:T(4,128)S(1)}, u32[]{:S(2)}, u32[]{:S(2)}) collective-permute-start(f32[1,2,4,64]{3,2,1,0:T(4,128)S(1)} %get-tuple-element.61), channel_id=1, source_target_pairs={{8,0},{16,8},{24,16},{0,24},{9,1},{17,9},{25,17},{1,25},{10,2},{18... | collective-permute-start | bytes 6152 | tf_op jit(solution)/shard_map/ppermute | solution.py:19
  99.2 6.3 %collective-permute-start.16 = (f32[1,1,4,64]{3,2,1,0:T(4,128)S(1)}, f32[1,1,4,64]{3,2,1,0:T(4,128)S(1)}, u32[]{:S(2)}, u32[]{:S(2)}) collective-permute-start(f32[1,1,4,64]{3,2,1,0:T(4,128)S(1)} %get-tuple-element.63), channel_id=1, source_target_pairs={{0,1},{1,2},{2,3},{3,4},{4,5},{5,6},{6,7},{7,0},{8,9},{9,10},{10,1... | collective-permute-start | bytes 3080 | tf_op jit(solution)/shard_map/ppermute | solution.py:17
  99.2 6.3 %collective-permute-start.17 = (f32[1,1,4,64]{3,2,1,0:T(4,128)S(1)}, f32[1,1,4,64]{3,2,1,0:T(4,128)S(1)}, u32[]{:S(2)}, u32[]{:S(2)}) collective-permute-start(f32[1,1,4,64]{3,2,1,0:T(4,128)S(1)} %get-tuple-element.64), channel_id=1, source_target_pairs={{1,0},{2,1},{3,2},{4,3},{5,4},{6,5},{7,6},{0,7},{9,8},{10,9},{11,1... | collective-permute-start | bytes 3080 | tf_op jit(solution)/shard_map/ppermute | solution.py:19
  136.8 6.5 %collective-permute-start.22 = (f32[1,2,4,64]{3,2,1,0:T(4,128)S(1)}, f32[1,2,4,64]{3,2,1,0:T(4,128)S(1)}, u32[]{:S(2)}, u32[]{:S(2)}) collective-permute-start(f32[1,2,4,64]{3,2,1,0:T(4,128)S(1)} %get-tuple-element.57), channel_id=1, source_target_pairs={{0,8},{8,16},{16,24},{24,0},{1,9},{9,17},{17,25},{25,1},{2,10},{10... | collective-permute-start | bytes 6152 | tf_op jit(solution)/shard_map/ppermute | solution.py:17
  136.8 8.0 %collective-permute-start.23 = (f32[1,2,4,64]{3,2,1,0:T(4,128)S(1)}, f32[1,2,4,64]{3,2,1,0:T(4,128)S(1)}, u32[]{:S(2)}, u32[]{:S(2)}) collective-permute-start(f32[1,2,4,64]{3,2,1,0:T(4,128)S(1)} %get-tuple-element.57), channel_id=1, source_target_pairs={{8,0},{16,8},{24,16},{0,24},{9,1},{17,9},{25,17},{1,25},{10,2},{18... | collective-permute-start | bytes 6152 | tf_op jit(solution)/shard_map/ppermute | solution.py:19
  138.6 6.3 %collective-permute-start.20 = (f32[1,1,4,64]{3,2,1,0:T(4,128)S(1)}, f32[1,1,4,64]{3,2,1,0:T(4,128)S(1)}, u32[]{:S(2)}, u32[]{:S(2)}) collective-permute-start(f32[1,1,4,64]{3,2,1,0:T(4,128)S(1)} %get-tuple-element.59), channel_id=1, source_target_pairs={{0,1},{1,2},{2,3},{3,4},{4,5},{5,6},{6,7},{7,0},{8,9},{9,10},{10,1... | collective-permute-start | bytes 3080 | tf_op jit(solution)/shard_map/ppermute | solution.py:17
  138.6 6.3 %collective-permute-start.21 = (f32[1,1,4,64]{3,2,1,0:T(4,128)S(1)}, f32[1,1,4,64]{3,2,1,0:T(4,128)S(1)}, u32[]{:S(2)}, u32[]{:S(2)}) collective-permute-start(f32[1,1,4,64]{3,2,1,0:T(4,128)S(1)} %get-tuple-element.60), channel_id=1, source_target_pairs={{1,0},{2,1},{3,2},{4,3},{5,4},{6,5},{7,6},{0,7},{9,8},{10,9},{11,1... | collective-permute-start | bytes 3080 | tf_op jit(solution)/shard_map/ppermute | solution.py:19
  195.1 6.5 %collective-permute-start.26 = (f32[1,2,4,64]{3,2,1,0:T(4,128)S(1)}, f32[1,2,4,64]{3,2,1,0:T(4,128)S(1)}, u32[]{:S(2)}, u32[]{:S(2)}) collective-permute-start(f32[1,2,4,64]{3,2,1,0:T(4,128)S(1)} %get-tuple-element.53), channel_id=1, source_target_pairs={{0,8},{8,16},{16,24},{24,0},{1,9},{9,17},{17,25},{25,1},{2,10},{10... | collective-permute-start | bytes 6152 | tf_op jit(solution)/shard_map/ppermute | solution.py:17
  195.1 8.0 %collective-permute-start.27 = (f32[1,2,4,64]{3,2,1,0:T(4,128)S(1)}, f32[1,2,4,64]{3,2,1,0:T(4,128)S(1)}, u32[]{:S(2)}, u32[]{:S(2)}) collective-permute-start(f32[1,2,4,64]{3,2,1,0:T(4,128)S(1)} %get-tuple-element.53), channel_id=1, source_target_pairs={{8,0},{16,8},{24,16},{0,24},{9,1},{17,9},{25,17},{1,25},{10,2},{18... | collective-permute-start | bytes 6152 | tf_op jit(solution)/shard_map/ppermute | solution.py:19
  196.8 6.3 %collective-permute-start.24 = (f32[1,1,4,64]{3,2,1,0:T(4,128)S(1)}, f32[1,1,4,64]{3,2,1,0:T(4,128)S(1)}, u32[]{:S(2)}, u32[]{:S(2)}) collective-permute-start(f32[1,1,4,64]{3,2,1,0:T(4,128)S(1)} %get-tuple-element.55), channel_id=1, source_target_pairs={{0,1},{1,2},{2,3},{3,4},{4,5},{5,6},{6,7},{7,0},{8,9},{9,10},{10,1... | collective-permute-start | bytes 3080 | tf_op jit(solution)/shard_map/ppermute | solution.py:17
  213.2 6.5 %collective-permute-start.30 = (f32[1,2,4,64]{3,2,1,0:T(4,128)S(1)}, f32[1,2,4,64]{3,2,1,0:T(4,128)S(1)}, u32[]{:S(2)}, u32[]{:S(2)}) collective-permute-start(f32[1,2,4,64]{3,2,1,0:T(4,128)S(1)} %get-tuple-element.49), channel_id=1, source_target_pairs={{0,8},{8,16},{16,24},{24,0},{1,9},{9,17},{17,25},{25,1},{2,10},{10... | collective-permute-start | bytes 6152 | tf_op jit(solution)/shard_map/ppermute | solution.py:17
  213.2 8.0 %collective-permute-start.31 = (f32[1,2,4,64]{3,2,1,0:T(4,128)S(1)}, f32[1,2,4,64]{3,2,1,0:T(4,128)S(1)}, u32[]{:S(2)}, u32[]{:S(2)}) collective-permute-start(f32[1,2,4,64]{3,2,1,0:T(4,128)S(1)} %get-tuple-element.49), channel_id=1, source_target_pairs={{8,0},{16,8},{24,16},{0,24},{9,1},{17,9},{25,17},{1,25},{10,2},{18... | collective-permute-start | bytes 6152 | tf_op jit(solution)/shard_map/ppermute | solution.py:19
  214.9 6.3 %collective-permute-start.28 = (f32[1,1,4,64]{3,2,1,0:T(4,128)S(1)}, f32[1,1,4,64]{3,2,1,0:T(4,128)S(1)}, u32[]{:S(2)}, u32[]{:S(2)}) collective-permute-start(f32[1,1,4,64]{3,2,1,0:T(4,128)S(1)} %get-tuple-element.51), channel_id=1, source_target_pairs={{0,1},{1,2},{2,3},{3,4},{4,5},{5,6},{6,7},{7,0},{8,9},{9,10},{10,1... | collective-permute-start | bytes 3080 | tf_op jit(solution)/shard_map/ppermute | solution.py:17
  231.0 6.5 %collective-permute-start.34 = (f32[1,2,4,64]{3,2,1,0:T(4,128)S(1)}, f32[1,2,4,64]{3,2,1,0:T(4,128)S(1)}, u32[]{:S(2)}, u32[]{:S(2)}) collective-permute-start(f32[1,2,4,64]{3,2,1,0:T(4,128)S(1)} %get-tuple-element.45), channel_id=1, source_target_pairs={{0,8},{8,16},{16,24},{24,0},{1,9},{9,17},{17,25},{25,1},{2,10},{10... | collective-permute-start | bytes 6152 | tf_op jit(solution)/shard_map/ppermute | solution.py:17
  231.0 8.0 %collective-permute-start.35 = (f32[1,2,4,64]{3,2,1,0:T(4,128)S(1)}, f32[1,2,4,64]{3,2,1,0:T(4,128)S(1)}, u32[]{:S(2)}, u32[]{:S(2)}) collective-permute-start(f32[1,2,4,64]{3,2,1,0:T(4,128)S(1)} %get-tuple-element.45), channel_id=1, source_target_pairs={{8,0},{16,8},{24,16},{0,24},{9,1},{17,9},{25,17},{1,25},{10,2},{18... | collective-permute-start | bytes 6152 | tf_op jit(solution)/shard_map/ppermute | solution.py:19
  232.8 6.3 %collective-permute-start.32 = (f32[1,1,4,64]{3,2,1,0:T(4,128)S(1)}, f32[1,1,4,64]{3,2,1,0:T(4,128)S(1)}, u32[]{:S(2)}, u32[]{:S(2)}) collective-permute-start(f32[1,1,4,64]{3,2,1,0:T(4,128)S(1)} %get-tuple-element.47), channel_id=1, source_target_pairs={{0,1},{1,2},{2,3},{3,4},{4,5},{5,6},{6,7},{7,0},{8,9},{9,10},{10,1... | collective-permute-start | bytes 3080 | tf_op jit(solution)/shard_map/ppermute | solution.py:17
  270.4 6.5 %collective-permute-start.38 = (f32[1,2,4,64]{3,2,1,0:T(4,128)S(1)}, f32[1,2,4,64]{3,2,1,0:T(4,128)S(1)}, u32[]{:S(2)}, u32[]{:S(2)}) collective-permute-start(f32[1,2,4,64]{3,2,1,0:T(4,128)S(1)} %get-tuple-element.41), channel_id=1, source_target_pairs={{0,8},{8,16},{16,24},{24,0},{1,9},{9,17},{17,25},{25,1},{2,10},{10... | collective-permute-start | bytes 6152 | tf_op jit(solution)/shard_map/ppermute | solution.py:17
  270.4 8.0 %collective-permute-start.39 = (f32[1,2,4,64]{3,2,1,0:T(4,128)S(1)}, f32[1,2,4,64]{3,2,1,0:T(4,128)S(1)}, u32[]{:S(2)}, u32[]{:S(2)}) collective-permute-start(f32[1,2,4,64]{3,2,1,0:T(4,128)S(1)} %get-tuple-element.41), channel_id=1, source_target_pairs={{8,0},{16,8},{24,16},{0,24},{9,1},{17,9},{25,17},{1,25},{10,2},{18... | collective-permute-start | bytes 6152 | tf_op jit(solution)/shard_map/ppermute | solution.py:19
  272.2 6.3 %collective-permute-start.36 = (f32[1,1,4,64]{3,2,1,0:T(4,128)S(1)}, f32[1,1,4,64]{3,2,1,0:T(4,128)S(1)}, u32[]{:S(2)}, u32[]{:S(2)}) collective-permute-start(f32[1,1,4,64]{3,2,1,0:T(4,128)S(1)} %get-tuple-element.43), channel_id=1, source_target_pairs={{0,1},{1,2},{2,3},{3,4},{4,5},{5,6},{6,7},{7,0},{8,9},{9,10},{10,1... | collective-permute-start | bytes 3080 | tf_op jit(solution)/shard_map/ppermute | solution.py:17
  272.2 6.3 %collective-permute-start.37 = (f32[1,1,4,64]{3,2,1,0:T(4,128)S(1)}, f32[1,1,4,64]{3,2,1,0:T(4,128)S(1)}, u32[]{:S(2)}, u32[]{:S(2)}) collective-permute-start(f32[1,1,4,64]{3,2,1,0:T(4,128)S(1)} %get-tuple-element.44), channel_id=1, source_target_pairs={{1,0},{2,1},{3,2},{4,3},{5,4},{6,5},{7,6},{0,7},{9,8},{10,9},{11,1... | collective-permute-start | bytes 3080 | tf_op jit(solution)/shard_map/ppermute | solution.py:19
  329.3 6.5 %collective-permute-start.42 = (f32[1,2,4,64]{3,2,1,0:T(4,128)S(1)}, f32[1,2,4,64]{3,2,1,0:T(4,128)S(1)}, u32[]{:S(2)}, u32[]{:S(2)}) collective-permute-start(f32[1,2,4,64]{3,2,1,0:T(4,128)S(1)} %get-tuple-element.37), channel_id=1, source_target_pairs={{0,8},{8,16},{16,24},{24,0},{1,9},{9,17},{17,25},{25,1},{2,10},{10... | collective-permute-start | bytes 6152 | tf_op jit(solution)/shard_map/ppermute | solution.py:17
  329.3 8.0 %collective-permute-start.43 = (f32[1,2,4,64]{3,2,1,0:T(4,128)S(1)}, f32[1,2,4,64]{3,2,1,0:T(4,128)S(1)}, u32[]{:S(2)}, u32[]{:S(2)}) collective-permute-start(f32[1,2,4,64]{3,2,1,0:T(4,128)S(1)} %get-tuple-element.37), channel_id=1, source_target_pairs={{8,0},{16,8},{24,16},{0,24},{9,1},{17,9},{25,17},{1,25},{10,2},{18... | collective-permute-start | bytes 6152 | tf_op jit(solution)/shard_map/ppermute | solution.py:19
  331.1 6.3 %collective-permute-start.40 = (f32[1,1,4,64]{3,2,1,0:T(4,128)S(1)}, f32[1,1,4,64]{3,2,1,0:T(4,128)S(1)}, u32[]{:S(2)}, u32[]{:S(2)}) collective-permute-start(f32[1,1,4,64]{3,2,1,0:T(4,128)S(1)} %get-tuple-element.39), channel_id=1, source_target_pairs={{0,1},{1,2},{2,3},{3,4},{4,5},{5,6},{6,7},{7,0},{8,9},{9,10},{10,1... | collective-permute-start | bytes 3080 | tf_op jit(solution)/shard_map/ppermute | solution.py:17
  347.4 6.5 %collective-permute-start.46 = (f32[1,2,4,64]{3,2,1,0:T(4,128)S(1)}, f32[1,2,4,64]{3,2,1,0:T(4,128)S(1)}, u32[]{:S(2)}, u32[]{:S(2)}) collective-permute-start(f32[1,2,4,64]{3,2,1,0:T(4,128)S(1)} %get-tuple-element.33), channel_id=1, source_target_pairs={{0,8},{8,16},{16,24},{24,0},{1,9},{9,17},{17,25},{25,1},{2,10},{10... | collective-permute-start | bytes 6152 | tf_op jit(solution)/shard_map/ppermute | solution.py:17
  347.4 8.0 %collective-permute-start.47 = (f32[1,2,4,64]{3,2,1,0:T(4,128)S(1)}, f32[1,2,4,64]{3,2,1,0:T(4,128)S(1)}, u32[]{:S(2)}, u32[]{:S(2)}) collective-permute-start(f32[1,2,4,64]{3,2,1,0:T(4,128)S(1)} %get-tuple-element.33), channel_id=1, source_target_pairs={{8,0},{16,8},{24,16},{0,24},{9,1},{17,9},{25,17},{1,25},{10,2},{18... | collective-permute-start | bytes 6152 | tf_op jit(solution)/shard_map/ppermute | solution.py:19
  349.2 6.3 %collective-permute-start.44 = (f32[1,1,4,64]{3,2,1,0:T(4,128)S(1)}, f32[1,1,4,64]{3,2,1,0:T(4,128)S(1)}, u32[]{:S(2)}, u32[]{:S(2)}) collective-permute-start(f32[1,1,4,64]{3,2,1,0:T(4,128)S(1)} %get-tuple-element.35), channel_id=1, source_target_pairs={{0,1},{1,2},{2,3},{3,4},{4,5},{5,6},{6,7},{7,0},{8,9},{9,10},{10,1... | collective-permute-start | bytes 3080 | tf_op jit(solution)/shard_map/ppermute | solution.py:17
  365.2 6.5 %collective-permute-start.50 = (f32[1,2,4,64]{3,2,1,0:T(4,128)S(1)}, f32[1,2,4,64]{3,2,1,0:T(4,128)S(1)}, u32[]{:S(2)}, u32[]{:S(2)}) collective-permute-start(f32[1,2,4,64]{3,2,1,0:T(4,128)S(1)} %get-tuple-element.29), channel_id=1, source_target_pairs={{0,8},{8,16},{16,24},{24,0},{1,9},{9,17},{17,25},{25,1},{2,10},{10... | collective-permute-start | bytes 6152 | tf_op jit(solution)/shard_map/ppermute | solution.py:17
  365.3 8.0 %collective-permute-start.51 = (f32[1,2,4,64]{3,2,1,0:T(4,128)S(1)}, f32[1,2,4,64]{3,2,1,0:T(4,128)S(1)}, u32[]{:S(2)}, u32[]{:S(2)}) collective-permute-start(f32[1,2,4,64]{3,2,1,0:T(4,128)S(1)} %get-tuple-element.29), channel_id=1, source_target_pairs={{8,0},{16,8},{24,16},{0,24},{9,1},{17,9},{25,17},{1,25},{10,2},{18... | collective-permute-start | bytes 6152 | tf_op jit(solution)/shard_map/ppermute | solution.py:19
  367.0 6.3 %collective-permute-start.48 = (f32[1,1,4,64]{3,2,1,0:T(4,128)S(1)}, f32[1,1,4,64]{3,2,1,0:T(4,128)S(1)}, u32[]{:S(2)}, u32[]{:S(2)}) collective-permute-start(f32[1,1,4,64]{3,2,1,0:T(4,128)S(1)} %get-tuple-element.31), channel_id=1, source_target_pairs={{0,1},{1,2},{2,3},{3,4},{4,5},{5,6},{6,7},{7,0},{8,9},{9,10},{10,1... | collective-permute-start | bytes 3080 | tf_op jit(solution)/shard_map/ppermute | solution.py:17
  404.6 6.5 %collective-permute-start.54 = (f32[1,2,4,64]{3,2,1,0:T(4,128)S(1)}, f32[1,2,4,64]{3,2,1,0:T(4,128)S(1)}, u32[]{:S(2)}, u32[]{:S(2)}) collective-permute-start(f32[1,2,4,64]{3,2,1,0:T(4,128)S(1)} %get-tuple-element.25), channel_id=1, source_target_pairs={{0,8},{8,16},{16,24},{24,0},{1,9},{9,17},{17,25},{25,1},{2,10},{10... | collective-permute-start | bytes 6152 | tf_op jit(solution)/shard_map/ppermute | solution.py:17
  404.7 8.0 %collective-permute-start.55 = (f32[1,2,4,64]{3,2,1,0:T(4,128)S(1)}, f32[1,2,4,64]{3,2,1,0:T(4,128)S(1)}, u32[]{:S(2)}, u32[]{:S(2)}) collective-permute-start(f32[1,2,4,64]{3,2,1,0:T(4,128)S(1)} %get-tuple-element.25), channel_id=1, source_target_pairs={{8,0},{16,8},{24,16},{0,24},{9,1},{17,9},{25,17},{1,25},{10,2},{18... | collective-permute-start | bytes 6152 | tf_op jit(solution)/shard_map/ppermute | solution.py:19
  406.4 6.3 %collective-permute-start.52 = (f32[1,1,4,64]{3,2,1,0:T(4,128)S(1)}, f32[1,1,4,64]{3,2,1,0:T(4,128)S(1)}, u32[]{:S(2)}, u32[]{:S(2)}) collective-permute-start(f32[1,1,4,64]{3,2,1,0:T(4,128)S(1)} %get-tuple-element.27), channel_id=1, source_target_pairs={{0,1},{1,2},{2,3},{3,4},{4,5},{5,6},{6,7},{7,0},{8,9},{9,10},{10,1... | collective-permute-start | bytes 3080 | tf_op jit(solution)/shard_map/ppermute | solution.py:17
  (14 other events, 97.7 us)
where the time goes:
time: 465 us; the launch traced here: 464 us
  blocking collectives  206 us (44%)
  local copies, waits for them, and re-layouts  139 us (30%)
  starting transfers between devices  92 us (20%)
  waiting for transfers between devices  20.7 us (4%)
    gather x14, local copies, waits for them, and re-layouts, jump(): picked = jnp.take_along_axis(facing, position, axis=-1)  134 us
    psum x3, blocking collectives, global_sums(): return lax.psum((first_dot, second_dot), ('srow', 'scol'))  122 us
    all_gather x4, blocking collectives, apply_inverse(): lax.all_gather(coarse_in, 'scol', axis=0, tiled=True)  84.1 us
    ppermute x28, starting transfers between devices, with_halo(): lax.ppermute(head, axis, [((i + 1) % count, i) for i in range(count)])  78.3 us
    ppermute x28, waiting for transfers between devices, with_halo(): lax.ppermute(tail, axis, [(i, (i + 1) % count) for i in range(count)])  20.7 us
    ppermute x28, starting transfers between devices, with_halo(): lax.ppermute(tail, axis, [(i, (i + 1) % count) for i in range(count)])  13.7 us
  transfers between devices with their start and end apart: 56, of which 14 were waited for; matrix products, arithmetic and copies ran while one was open for 0% of the time, Pallas kernels for 0%

commit v1 on v0

--- a/solution.py
+++ b/solution.py
@@ -5,6 +5,22 @@
 
 ITERS = 3
 precise = lax.Precision.HIGHEST
+
+
+def gather_around(x, axis, dim):
+    ways, here, hop = (lax.axis_size(axis), lax.axis_index(axis), x.shape[dim])
+    shape = [n * ways if d == dim else n for d, n in enumerate(x.shape)]
+    full = lax.dynamic_update_slice_in_dim(jnp.zeros(shape, x.dtype), x, here * hop, axis=dim)
+    going_up = going_down = x
+    for far in range(1, ways // 2 + 1):
+        going_up = lax.ppermute(going_up, axis, [(d, (d + 1) % ways) for d in range(ways)])
+        full = lax.dynamic_update_slice_in_dim(full, going_up, (here - far) % ways * hop, axis=dim)
+        if 2 * far < ways:
+            going_down = lax.ppermute(going_down, axis, [(d, (d - 1) % ways) for d in range(ways)])
+            full = lax.dynamic_update_slice_in_dim(
+                full, going_down, (here + far) % ways * hop, axis=dim
+            )
+    return full
 
 
 def with_halo(cells, sides, width):
@@ -52,7 +68,7 @@
     band_rows = coarse_inverse[0]
     coarse_out = jnp.dot(
         band_rows,
-        lax.all_gather(coarse_in, "scol", axis=0, tiled=True),
+        gather_around(coarse_in, "scol", 0),
         precision=precise,
         preferred_element_type=jnp.float32,
     )

time: 465 us -> 480 us (1.032)
  blocking collectives: 206 us -> 122 us
  starting transfers between devices: 92 us -> 149 us
  waiting for transfers between devices: 20.7 us -> 63.4 us
    all_gather x4 -> x0, blocking collectives: 84.1 us -> none  [apply_inverse(): lax.all_gather(coarse_in, 'scol', axis=0, tiled=True)]
    ppermute x0 -> x28, starting transfers between devices: none -> 56.8 us  [the longest x12 55 us: gather_around(): lax.ppermute(going_down, axis, [(d, (d - 1) % ways) for d in range(ways)])]
    ppermute x0 -> x28, waiting for transfers between devices: none -> 43.4 us  [the longest x16 43.3 us: gather_around(): lax.ppermute(going_up, axis, [(d, (d + 1) % ways) for d in range(ways)])]
  transfers between devices with their start and end apart: 56 -> 84, of which waited for: 14 -> 30; matrix products, arithmetic and copies ran while one was open for 0% -> 0% of each run, Pallas kernels for 0% -> 0%
where the time goes in v1:
time: 480 us
  starting transfers between devices  149 us (31%)
  local copies, waits for them, and re-layouts  139 us (29%)
  blocking collectives  122 us (25%)
  waiting for transfers between devices  63.4 us (13%)
    gather x14, local copies, waits for them, and re-layouts, jump(): picked = jnp.take_along_axis(facing, position, axis=-1)  134 us
    psum x3, blocking collectives, global_sums(): return lax.psum((first_dot, second_dot), ('srow', 'scol'))  122 us
    ppermute x28, starting transfers between devices, with_halo(): lax.ppermute(head, axis, [((i + 1) % count, i) for i in range(count)])  78.3 us
    ppermute x12, starting transfers between devices, gather_around(): lax.ppermute(going_down, axis, [(d, (d - 1) % ways) for d in range(ways)])  55 us
    ppermute x16, waiting for transfers between devices, gather_around(): lax.ppermute(going_up, axis, [(d, (d + 1) % ways) for d in range(ways)])  43.3 us
    ppermute x28, waiting for transfers between devices, with_halo(): lax.ppermute(tail, axis, [(i, (i + 1) % count) for i in range(count)])  19.9 us
    ppermute x28, starting transfers between devices, with_halo(): lax.ppermute(tail, axis, [(i, (i + 1) % count) for i in range(count)])  13.7 us
  transfers between devices with their start and end apart: 84, of which 30 were waited for; matrix products, arithmetic and copies ran while one was open for 0% of the time, Pallas kernels for 0%

profile of v1, /device:TPU:0, one launch (start us, length us, event | category | flops | bytes accessed | tf_op | source)
XLA Modules:
  0.0 479.8 jit_solution(257551321463149300)
XLA Ops:
  6.2 3.1 collective-permute-start.1
  10.9 9.6 %gather_fusion = f32[1024]{0:T(1024)S(1)} fusion(f32[2,4,128]{2,1,0:T(4,128)S(1)} %fusion.69, s32[1024]{0:T(1024)S(1)} %bitcast.204), kind=kCustom, calls=%fused_computation.clone | custom fusion | bytes 20480 | tf_op jit(solution)/shard_map/jit(take_along_axis)/gather | solution.py:59
  22.8 3.3 collective-permute-start.5
  27.7 4.7 collective-permute-start.7
  34.0 4.7 collective-permute-start.9
  40.3 6.2 %collective-permute-done.10 = f32[2,4]{1,0:T(2,128)S(1)} collective-permute-done((f32[2,4]{1,0:T(2,128)S(1)}, f32[2,4]{1,0:T(2,128)S(1)}, u32[]{:S(2)}, u32[]{:S(2)}) %collective-permute-start.10) | collective-permute-done | bytes 64 | tf_op jit(solution)/shard_map/ppermute | solution.py:16
  48.8 4.7 collective-permute-start.12
  55.2 9.6 %gather_fusion.1 = f32[1024]{0:T(1024)S(1)} fusion(f32[2,4,128]{2,1,0:T(4,128)S(1)} %fusion.65, s32[1024]{0:T(1024)S(1)} %bitcast.205), kind=kCustom, calls=%fused_computation.1.clone | custom fusion | bytes 20480 | tf_op jit(solution)/shard_map/jit(take_along_axis)/gather | solution.py:59
  66.6 4.7 collective-permute-start.16
  73.0 9.6 %gather_fusion.2 = f32[1024]{0:T(1024)S(1)} fusion(f32[2,4,128]{2,1,0:T(4,128)S(1)} %fusion.61, s32[1024]{0:T(1024)S(1)} %bitcast.206), kind=kCustom, calls=%fused_computation.2.clone | custom fusion | bytes 20480 | tf_op jit(solution)/shard_map/jit(take_along_axis)/gather | solution.py:59
  84.8 4.7 collective-permute-start.20
  91.1 9.6 %gather_fusion.3 = f32[1024]{0:T(1024)S(1)} fusion(f32[2,4,128]{2,1,0:T(4,128)S(1)} %fusion.57, s32[1024]{0:T(1024)S(1)} %bitcast.207), kind=kCustom, calls=%fused_computation.3.clone | custom fusion | bytes 20480 | tf_op jit(solution)/shard_map/jit(take_along_axis)/gather | solution.py:59
  102.6 4.7 collective-permute-start.24
  108.9 9.6 %gather_fusion.4 = f32[1024]{0:T(1024)S(1)} fusion(f32[2,4,128]{2,1,0:T(4,128)S(1)} %fusion.53, s32[1024]{0:T(1024)S(1)} %bitcast.208), kind=kCustom, calls=%fused_computation.4.clone | custom fusion | bytes 20480 | tf_op jit(solution)/shard_map/jit(take_along_axis)/gather | solution.py:59
  118.7 4.7 collective-permute-start.28
  125.0 4.7 collective-permute-start.30
  131.3 4.7 collective-permute-start.32
  137.6 6.2 %collective-permute-done.33 = f32[2,4]{1,0:T(2,128)S(1)} collective-permute-done((f32[2,4]{1,0:T(2,128)S(1)}, f32[2,4]{1,0:T(2,128)S(1)}, u32[]{:S(2)}, u32[]{:S(2)}) %collective-permute-start.33) | collective-permute-done | bytes 64 | tf_op jit(solution)/shard_map/ppermute | solution.py:16
  146.1 4.7 collective-permute-start.35
  152.5 9.6 %gather_fusion.5 = f32[1024]{0:T(1024)S(1)} fusion(f32[2,4,128]{2,1,0:T(4,128)S(1)} %fusion.49, s32[1024]{0:T(1024)S(1)} %bitcast.209), kind=kCustom, calls=%fused_computation.5.clone | custom fusion | bytes 20480 | tf_op jit(solution)/shard_map/jit(take_along_axis)/gather | solution.py:59
  162.2 40.2 %all-reduce.2 = (f32[4]{0:T(128)S(1)}, f32[4]{0:T(128)S(1)}) all-reduce(f32[4]{0:T(128)S(1)} %get-tuple-element.8, f32[4]{0:T(128)S(1)} %get-tuple-element.7), channel_id=1, replica_groups=mesh['srow'=4,'scol'=8] {'srow','scol'}, use_global_device_ids=true, to_apply=%region_1.3 | all-reduce | flops 8 | bytes 64 | tf_op jit(solution)/shard_map/psum | solution.py:84
  204.4 2.3 collective-permute-start.38
  206.6 2.4 collective-permute-start.39
  210.7 9.6 %gather_fusion.6 = f32[1024]{0:T(1024)S(1)} fusion(f32[2,4,128]{2,1,0:T(4,128)S(1)} %fusion.45, s32[1024]{0:T(1024)S(1)} %bitcast.210), kind=kCustom, calls=%fused_computation.6.clone | custom fusion | bytes 20480 | tf_op jit(solution)/shard_map/jit(take_along_axis)/gather | solution.py:59
  224.3 2.9 collective-permute-start.43
  228.8 9.6 %gather_fusion.7 = f32[1024]{0:T(1024)S(1)} fusion(f32[2,4,128]{2,1,0:T(4,128)S(1)} %fusion.41, s32[1024]{0:T(1024)S(1)} %bitcast.211), kind=kCustom, calls=%fused_computation.7.clone | custom fusion | bytes 20480 | tf_op jit(solution)/shard_map/jit(take_along_axis)/gather | solution.py:59
  241.7 3.4 collective-permute-start.47
  246.7 9.6 %gather_fusion.8 = f32[1024]{0:T(1024)S(1)} fusion(f32[2,4,128]{2,1,0:T(4,128)S(1)} %fusion.37, s32[1024]{0:T(1024)S(1)} %bitcast.212), kind=kCustom, calls=%fused_computation.8.clone | custom fusion | bytes 20480 | tf_op jit(solution)/shard_map/jit(take_along_axis)/gather | solution.py:59
  256.6 4.6 collective-permute-start.51
  262.7 4.7 collective-permute-start.53
  269.0 4.7 collective-permute-start.55
  275.3 6.2 %collective-permute-done.56 = f32[2,4]{1,0:T(2,128)S(1)} collective-permute-done((f32[2,4]{1,0:T(2,128)S(1)}, f32[2,4]{1,0:T(2,128)S(1)}, u32[]{:S(2)}, u32[]{:S(2)}) %collective-permute-start.56) | collective-permute-done | bytes 64 | tf_op jit(solution)/shard_map/ppermute | solution.py:16
  283.8 4.7 collective-permute-start.58
  290.2 9.6 %gather_fusion.9 = f32[1024]{0:T(1024)S(1)} fusion(f32[2,4,128]{2,1,0:T(4,128)S(1)} %fusion.33, s32[1024]{0:T(1024)S(1)} %bitcast.213), kind=kCustom, calls=%fused_computation.9.clone | custom fusion | bytes 20480 | tf_op jit(solution)/shard_map/jit(take_along_axis)/gather | solution.py:59
  299.9 40.8 %all-reduce.1 = (f32[4]{0:T(128)S(1)}, f32[4]{0:T(128)S(1)}) all-reduce(f32[4]{0:T(128)S(1)} %get-tuple-element.6, f32[4]{0:T(128)S(1)} %get-tuple-element.5), channel_id=1, replica_groups=mesh['srow'=4,'scol'=8] {'srow','scol'}, use_global_device_ids=true, to_apply=%region_5.7 | all-reduce | flops 8 | bytes 64 | tf_op jit(solution)/shard_map/psum | solution.py:84
  345.0 2.4 collective-permute-start.62
  349.1 9.6 %gather_fusion.10 = f32[1024]{0:T(1024)S(1)} fusion(f32[2,4,128]{2,1,0:T(4,128)S(1)} %fusion.29, s32[1024]{0:T(1024)S(1)} %bitcast.214), kind=kCustom, calls=%fused_computation.10.clone | custom fusion | bytes 20480 | tf_op jit(solution)/shard_map/jit(take_along_axis)/gather | solution.py:59
  362.6 2.9 collective-permute-start.66
  367.2 9.6 %gather_fusion.11 = f32[1024]{0:T(1024)S(1)} fusion(f32[2,4,128]{2,1,0:T(4,128)S(1)} %fusion.25, s32[1024]{0:T(1024)S(1)} %bitcast.215), kind=kCustom, calls=%fused_computation.11.clone | custom fusion | bytes 20480 | tf_op jit(solution)/shard_map/jit(take_along_axis)/gather | solution.py:59
  380.0 3.4 collective-permute-start.70
  385.0 9.6 %gather_fusion.12 = f32[1024]{0:T(1024)S(1)} fusion(f32[2,4,128]{2,1,0:T(4,128)S(1)} %fusion.21, s32[1024]{0:T(1024)S(1)} %bitcast.216), kind=kCustom, calls=%fused_computation.12.clone | custom fusion | bytes 20480 | tf_op jit(solution)/shard_map/jit(take_along_axis)/gather | solution.py:59
  394.9 4.6 collective-permute-start.74
  401.1 4.7 collective-permute-start.76
  407.3 4.7 collective-permute-start.78
  413.6 6.2 %collective-permute-done.79 = f32[2,4]{1,0:T(2,128)S(1)} collective-permute-done((f32[2,4]{1,0:T(2,128)S(1)}, f32[2,4]{1,0:T(2,128)S(1)}, u32[]{:S(2)}, u32[]{:S(2)}) %collective-permute-start.79) | collective-permute-done | bytes 64 | tf_op jit(solution)/shard_map/ppermute | solution.py:16
  422.2 4.7 collective-permute-start.81
  428.5 9.6 %gather_fusion.13 = f32[1024]{0:T(1024)S(1)} fusion(f32[2,4,128]{2,1,0:T(4,128)S(1)} %fusion.17, s32[1024]{0:T(1024)S(1)} %bitcast.217), kind=kCustom, calls=%fused_computation.13.clone | custom fusion | bytes 20480 | tf_op jit(solution)/shard_map/jit(take_along_axis)/gather | solution.py:59
  438.3 40.8 %all-reduce = (f32[4]{0:T(128)S(1)}, f32[4]{0:T(128)S(1)}) all-reduce(f32[4]{0:T(128)S(1)} %get-tuple-element.4, f32[4]{0:T(128)S(1)} %get-tuple-element.3), channel_id=1, replica_groups=mesh['srow'=4,'scol'=8] {'srow','scol'}, use_global_device_ids=true, to_apply=%region_9.11 | all-reduce | flops 8 | bytes 64 | tf_op jit(solution)/shard_map/psum | solution.py:84
  (275 shorter events, 86.4 us)
Async XLA Ops:
  1.5 8.6 %collective-permute-start.2 = (f32[1,2,4,64]{3,2,1,0:T(4,128)S(1)}, f32[1,2,4,64]{3,2,1,0:T(4,128)S(1)}, u32[]{:S(2)}, u32[]{:S(2)}) collective-permute-start(f32[1,2,4,64]{3,2,1,0:T(4,128)S(1)} %get-tuple-element.77), channel_id=1, source_target_pairs={{0,8},{8,16},{16,24},{24,0},{1,9},{9,17},{17,25},{25,1},{2,10},{10... | collective-permute-start | bytes 6152 | tf_op jit(solution)/shard_map/ppermute | solution.py:33
  2.0 8.8 %collective-permute-start.3 = (f32[1,2,4,64]{3,2,1,0:T(4,128)S(1)}, f32[1,2,4,64]{3,2,1,0:T(4,128)S(1)}, u32[]{:S(2)}, u32[]{:S(2)}) collective-permute-start(f32[1,2,4,64]{3,2,1,0:T(4,128)S(1)} %get-tuple-element.77), channel_id=1, source_target_pairs={{8,0},{16,8},{24,16},{0,24},{9,1},{17,9},{25,17},{1,25},{10,2},{18... | collective-permute-start | bytes 6152 | tf_op jit(solution)/shard_map/ppermute | solution.py:35
  4.0 6.9 %collective-permute-start = (f32[1,1,4,64]{3,2,1,0:T(4,128)S(1)}, f32[1,1,4,64]{3,2,1,0:T(4,128)S(1)}, u32[]{:S(2)}, u32[]{:S(2)}) collective-permute-start(f32[1,1,4,64]{3,2,1,0:T(4,128)S(1)} %get-tuple-element.79), channel_id=1, source_target_pairs={{0,1},{1,2},{2,3},{3,4},{4,5},{5,6},{6,7},{7,0},{8,9},{9,10},{10,1... | collective-permute-start | bytes 3080 | tf_op jit(solution)/shard_map/ppermute | solution.py:33
  21.3 6.3 %collective-permute-start.4 = (f32[2,4]{1,0:T(2,128)S(1)}, f32[2,4]{1,0:T(2,128)S(1)}, u32[]{:S(2)}, u32[]{:S(2)}) collective-permute-start(f32[2,4]{1,0:T(2,128)S(1)} %bitcast.269), channel_id=1, source_target_pairs={{0,1},{1,2},{2,3},{3,4},{4,5},{5,6},{6,7},{7,0},{8,9},{9,10},{10,1... | collective-permute-start | bytes 104 | tf_op jit(solution)/shard_map/ppermute | solution.py:16
  47.0 6.5 %collective-permute-start.13 = (f32[1,2,4,64]{3,2,1,0:T(4,128)S(1)}, f32[1,2,4,64]{3,2,1,0:T(4,128)S(1)}, u32[]{:S(2)}, u32[]{:S(2)}) collective-permute-start(f32[1,2,4,64]{3,2,1,0:T(4,128)S(1)} %get-tuple-element.73), channel_id=1, source_target_pairs={{0,8},{8,16},{16,24},{24,0},{1,9},{9,17},{17,25},{25,1},{2,10},{10... | collective-permute-start | bytes 6152 | tf_op jit(solution)/shard_map/ppermute | solution.py:33
  47.0 8.0 %collective-permute-start.14 = (f32[1,2,4,64]{3,2,1,0:T(4,128)S(1)}, f32[1,2,4,64]{3,2,1,0:T(4,128)S(1)}, u32[]{:S(2)}, u32[]{:S(2)}) collective-permute-start(f32[1,2,4,64]{3,2,1,0:T(4,128)S(1)} %get-tuple-element.73), channel_id=1, source_target_pairs={{8,0},{16,8},{24,16},{0,24},{9,1},{17,9},{25,17},{1,25},{10,2},{18... | collective-permute-start | bytes 6152 | tf_op jit(solution)/shard_map/ppermute | solution.py:35
  48.8 6.3 %collective-permute-start.11 = (f32[1,1,4,64]{3,2,1,0:T(4,128)S(1)}, f32[1,1,4,64]{3,2,1,0:T(4,128)S(1)}, u32[]{:S(2)}, u32[]{:S(2)}) collective-permute-start(f32[1,1,4,64]{3,2,1,0:T(4,128)S(1)} %get-tuple-element.75), channel_id=1, source_target_pairs={{0,1},{1,2},{2,3},{3,4},{4,5},{5,6},{6,7},{7,0},{8,9},{9,10},{10,1... | collective-permute-start | bytes 3080 | tf_op jit(solution)/shard_map/ppermute | solution.py:33
  48.8 6.3 %collective-permute-start.12 = (f32[1,1,4,64]{3,2,1,0:T(4,128)S(1)}, f32[1,1,4,64]{3,2,1,0:T(4,128)S(1)}, u32[]{:S(2)}, u32[]{:S(2)}) collective-permute-start(f32[1,1,4,64]{3,2,1,0:T(4,128)S(1)} %get-tuple-element.76), channel_id=1, source_target_pairs={{1,0},{2,1},{3,2},{4,3},{5,4},{6,5},{7,6},{0,7},{9,8},{10,9},{11,1... | collective-permute-start | bytes 3080 | tf_op jit(solution)/shard_map/ppermute | solution.py:35
  64.9 6.5 %collective-permute-start.17 = (f32[1,2,4,64]{3,2,1,0:T(4,128)S(1)}, f32[1,2,4,64]{3,2,1,0:T(4,128)S(1)}, u32[]{:S(2)}, u32[]{:S(2)}) collective-permute-start(f32[1,2,4,64]{3,2,1,0:T(4,128)S(1)} %get-tuple-element.69), channel_id=1, source_target_pairs={{0,8},{8,16},{16,24},{24,0},{1,9},{9,17},{17,25},{25,1},{2,10},{10... | collective-permute-start | bytes 6152 | tf_op jit(solution)/shard_map/ppermute | solution.py:33
  64.9 8.0 %collective-permute-start.18 = (f32[1,2,4,64]{3,2,1,0:T(4,128)S(1)}, f32[1,2,4,64]{3,2,1,0:T(4,128)S(1)}, u32[]{:S(2)}, u32[]{:S(2)}) collective-permute-start(f32[1,2,4,64]{3,2,1,0:T(4,128)S(1)} %get-tuple-element.69), channel_id=1, source_target_pairs={{8,0},{16,8},{24,16},{0,24},{9,1},{17,9},{25,17},{1,25},{10,2},{18... | collective-permute-start | bytes 6152 | tf_op jit(solution)/shard_map/ppermute | solution.py:35
  66.6 6.3 %collective-permute-start.15 = (f32[1,1,4,64]{3,2,1,0:T(4,128)S(1)}, f32[1,1,4,64]{3,2,1,0:T(4,128)S(1)}, u32[]{:S(2)}, u32[]{:S(2)}) collective-permute-start(f32[1,1,4,64]{3,2,1,0:T(4,128)S(1)} %get-tuple-element.71), channel_id=1, source_target_pairs={{0,1},{1,2},{2,3},{3,4},{4,5},{5,6},{6,7},{7,0},{8,9},{9,10},{10,1... | collective-permute-start | bytes 3080 | tf_op jit(solution)/shard_map/ppermute | solution.py:33
  66.6 6.3 %collective-permute-start.16 = (f32[1,1,4,64]{3,2,1,0:T(4,128)S(1)}, f32[1,1,4,64]{3,2,1,0:T(4,128)S(1)}, u32[]{:S(2)}, u32[]{:S(2)}) collective-permute-start(f32[1,1,4,64]{3,2,1,0:T(4,128)S(1)} %get-tuple-element.72), channel_id=1, source_target_pairs={{1,0},{2,1},{3,2},{4,3},{5,4},{6,5},{7,6},{0,7},{9,8},{10,9},{11,1... | collective-permute-start | bytes 3080 | tf_op jit(solution)/shard_map/ppermute | solution.py:35
  83.0 6.5 %collective-permute-start.21 = (f32[1,2,4,64]{3,2,1,0:T(4,128)S(1)}, f32[1,2,4,64]{3,2,1,0:T(4,128)S(1)}, u32[]{:S(2)}, u32[]{:S(2)}) collective-permute-start(f32[1,2,4,64]{3,2,1,0:T(4,128)S(1)} %get-tuple-element.65), channel_id=1, source_target_pairs={{0,8},{8,16},{16,24},{24,0},{1,9},{9,17},{17,25},{25,1},{2,10},{10... | collective-permute-start | bytes 6152 | tf_op jit(solution)/shard_map/ppermute | solution.py:33
  83.0 8.0 %collective-permute-start.22 = (f32[1,2,4,64]{3,2,1,0:T(4,128)S(1)}, f32[1,2,4,64]{3,2,1,0:T(4,128)S(1)}, u32[]{:S(2)}, u32[]{:S(2)}) collective-permute-start(f32[1,2,4,64]{3,2,1,0:T(4,128)S(1)} %get-tuple-element.65), channel_id=1, source_target_pairs={{8,0},{16,8},{24,16},{0,24},{9,1},{17,9},{25,17},{1,25},{10,2},{18... | collective-permute-start | bytes 6152 | tf_op jit(solution)/shard_map/ppermute | solution.py:35
  84.8 6.3 %collective-permute-start.19 = (f32[1,1,4,64]{3,2,1,0:T(4,128)S(1)}, f32[1,1,4,64]{3,2,1,0:T(4,128)S(1)}, u32[]{:S(2)}, u32[]{:S(2)}) collective-permute-start(f32[1,1,4,64]{3,2,1,0:T(4,128)S(1)} %get-tuple-element.67), channel_id=1, source_target_pairs={{0,1},{1,2},{2,3},{3,4},{4,5},{5,6},{6,7},{7,0},{8,9},{9,10},{10,1... | collective-permute-start | bytes 3080 | tf_op jit(solution)/shard_map/ppermute | solution.py:33
  84.8 6.3 %collective-permute-start.20 = (f32[1,1,4,64]{3,2,1,0:T(4,128)S(1)}, f32[1,1,4,64]{3,2,1,0:T(4,128)S(1)}, u32[]{:S(2)}, u32[]{:S(2)}) collective-permute-start(f32[1,1,4,64]{3,2,1,0:T(4,128)S(1)} %get-tuple-element.68), channel_id=1, source_target_pairs={{1,0},{2,1},{3,2},{4,3},{5,4},{6,5},{7,6},{0,7},{9,8},{10,9},{11,1... | collective-permute-start | bytes 3080 | tf_op jit(solution)/shard_map/ppermute | solution.py:35
  100.8 6.5 %collective-permute-start.25 = (f32[1,2,4,64]{3,2,1,0:T(4,128)S(1)}, f32[1,2,4,64]{3,2,1,0:T(4,128)S(1)}, u32[]{:S(2)}, u32[]{:S(2)}) collective-permute-start(f32[1,2,4,64]{3,2,1,0:T(4,128)S(1)} %get-tuple-element.61), channel_id=1, source_target_pairs={{0,8},{8,16},{16,24},{24,0},{1,9},{9,17},{17,25},{25,1},{2,10},{10... | collective-permute-start | bytes 6152 | tf_op jit(solution)/shard_map/ppermute | solution.py:33
  100.8 8.0 %collective-permute-start.26 = (f32[1,2,4,64]{3,2,1,0:T(4,128)S(1)}, f32[1,2,4,64]{3,2,1,0:T(4,128)S(1)}, u32[]{:S(2)}, u32[]{:S(2)}) collective-permute-start(f32[1,2,4,64]{3,2,1,0:T(4,128)S(1)} %get-tuple-element.61), channel_id=1, source_target_pairs={{8,0},{16,8},{24,16},{0,24},{9,1},{17,9},{25,17},{1,25},{10,2},{18... | collective-permute-start | bytes 6152 | tf_op jit(solution)/shard_map/ppermute | solution.py:35
  102.6 6.3 %collective-permute-start.23 = (f32[1,1,4,64]{3,2,1,0:T(4,128)S(1)}, f32[1,1,4,64]{3,2,1,0:T(4,128)S(1)}, u32[]{:S(2)}, u32[]{:S(2)}) collective-permute-start(f32[1,1,4,64]{3,2,1,0:T(4,128)S(1)} %get-tuple-element.63), channel_id=1, source_target_pairs={{0,1},{1,2},{2,3},{3,4},{4,5},{5,6},{6,7},{7,0},{8,9},{9,10},{10,1... | collective-permute-start | bytes 3080 | tf_op jit(solution)/shard_map/ppermute | solution.py:33
  102.6 6.3 %collective-permute-start.24 = (f32[1,1,4,64]{3,2,1,0:T(4,128)S(1)}, f32[1,1,4,64]{3,2,1,0:T(4,128)S(1)}, u32[]{:S(2)}, u32[]{:S(2)}) collective-permute-start(f32[1,1,4,64]{3,2,1,0:T(4,128)S(1)} %get-tuple-element.64), channel_id=1, source_target_pairs={{1,0},{2,1},{3,2},{4,3},{5,4},{6,5},{7,6},{0,7},{9,8},{10,9},{11,1... | collective-permute-start | bytes 3080 | tf_op jit(solution)/shard_map/ppermute | solution.py:35
  118.7 6.3 %collective-permute-start.27 = (f32[2,4]{1,0:T(2,128)S(1)}, f32[2,4]{1,0:T(2,128)S(1)}, u32[]{:S(2)}, u32[]{:S(2)}) collective-permute-start(f32[2,4]{1,0:T(2,128)S(1)} %bitcast.263), channel_id=1, source_target_pairs={{0,1},{1,2},{2,3},{3,4},{4,5},{5,6},{6,7},{7,0},{8,9},{9,10},{10,1... | collective-permute-start | bytes 104 | tf_op jit(solution)/shard_map/ppermute | solution.py:16
  118.7 6.3 %collective-permute-start.28 = (f32[2,4]{1,0:T(2,128)S(1)}, f32[2,4]{1,0:T(2,128)S(1)}, u32[]{:S(2)}, u32[]{:S(2)}) collective-permute-start(f32[2,4]{1,0:T(2,128)S(1)} %bitcast.264), channel_id=1, source_target_pairs={{0,7},{1,0},{2,1},{3,2},{4,3},{5,4},{6,5},{7,6},{8,15},{9,8},{10,9... | collective-permute-start | bytes 104 | tf_op jit(solution)/shard_map/ppermute | solution.py:19
  144.3 6.5 %collective-permute-start.36 = (f32[1,2,4,64]{3,2,1,0:T(4,128)S(1)}, f32[1,2,4,64]{3,2,1,0:T(4,128)S(1)}, u32[]{:S(2)}, u32[]{:S(2)}) collective-permute-start(f32[1,2,4,64]{3,2,1,0:T(4,128)S(1)} %get-tuple-element.57), channel_id=1, source_target_pairs={{0,8},{8,16},{16,24},{24,0},{1,9},{9,17},{17,25},{25,1},{2,10},{10... | collective-permute-start | bytes 6152 | tf_op jit(solution)/shard_map/ppermute | solution.py:33
  144.3 8.0 %collective-permute-start.37 = (f32[1,2,4,64]{3,2,1,0:T(4,128)S(1)}, f32[1,2,4,64]{3,2,1,0:T(4,128)S(1)}, u32[]{:S(2)}, u32[]{:S(2)}) collective-permute-start(f32[1,2,4,64]{3,2,1,0:T(4,128)S(1)} %get-tuple-element.57), channel_id=1, source_target_pairs={{8,0},{16,8},{24,16},{0,24},{9,1},{17,9},{25,17},{1,25},{10,2},{18... | collective-permute-start | bytes 6152 | tf_op jit(solution)/shard_map/ppermute | solution.py:35
  146.1 6.3 %collective-permute-start.34 = (f32[1,1,4,64]{3,2,1,0:T(4,128)S(1)}, f32[1,1,4,64]{3,2,1,0:T(4,128)S(1)}, u32[]{:S(2)}, u32[]{:S(2)}) collective-permute-start(f32[1,1,4,64]{3,2,1,0:T(4,128)S(1)} %get-tuple-element.59), channel_id=1, source_target_pairs={{0,1},{1,2},{2,3},{3,4},{4,5},{5,6},{6,7},{7,0},{8,9},{9,10},{10,1... | collective-permute-start | bytes 3080 | tf_op jit(solution)/shard_map/ppermute | solution.py:33
  146.1 6.3 %collective-permute-start.35 = (f32[1,1,4,64]{3,2,1,0:T(4,128)S(1)}, f32[1,1,4,64]{3,2,1,0:T(4,128)S(1)}, u32[]{:S(2)}, u32[]{:S(2)}) collective-permute-start(f32[1,1,4,64]{3,2,1,0:T(4,128)S(1)} %get-tuple-element.60), channel_id=1, source_target_pairs={{1,0},{2,1},{3,2},{4,3},{5,4},{6,5},{7,6},{0,7},{9,8},{10,9},{11,1... | collective-permute-start | bytes 3080 | tf_op jit(solution)/shard_map/ppermute | solution.py:35
  202.6 6.5 %collective-permute-start.40 = (f32[1,2,4,64]{3,2,1,0:T(4,128)S(1)}, f32[1,2,4,64]{3,2,1,0:T(4,128)S(1)}, u32[]{:S(2)}, u32[]{:S(2)}) collective-permute-start(f32[1,2,4,64]{3,2,1,0:T(4,128)S(1)} %get-tuple-element.53), channel_id=1, source_target_pairs={{0,8},{8,16},{16,24},{24,0},{1,9},{9,17},{17,25},{25,1},{2,10},{10... | collective-permute-start | bytes 6152 | tf_op jit(solution)/shard_map/ppermute | solution.py:33
  202.6 8.0 %collective-permute-start.41 = (f32[1,2,4,64]{3,2,1,0:T(4,128)S(1)}, f32[1,2,4,64]{3,2,1,0:T(4,128)S(1)}, u32[]{:S(2)}, u32[]{:S(2)}) collective-permute-start(f32[1,2,4,64]{3,2,1,0:T(4,128)S(1)} %get-tuple-element.53), channel_id=1, source_target_pairs={{8,0},{16,8},{24,16},{0,24},{9,1},{17,9},{25,17},{1,25},{10,2},{18... | collective-permute-start | bytes 6152 | tf_op jit(solution)/shard_map/ppermute | solution.py:35
  220.7 6.5 %collective-permute-start.44 = (f32[1,2,4,64]{3,2,1,0:T(4,128)S(1)}, f32[1,2,4,64]{3,2,1,0:T(4,128)S(1)}, u32[]{:S(2)}, u32[]{:S(2)}) collective-permute-start(f32[1,2,4,64]{3,2,1,0:T(4,128)S(1)} %get-tuple-element.49), channel_id=1, source_target_pairs={{0,8},{8,16},{16,24},{24,0},{1,9},{9,17},{17,25},{25,1},{2,10},{10... | collective-permute-start | bytes 6152 | tf_op jit(solution)/shard_map/ppermute | solution.py:33
  220.7 8.0 %collective-permute-start.45 = (f32[1,2,4,64]{3,2,1,0:T(4,128)S(1)}, f32[1,2,4,64]{3,2,1,0:T(4,128)S(1)}, u32[]{:S(2)}, u32[]{:S(2)}) collective-permute-start(f32[1,2,4,64]{3,2,1,0:T(4,128)S(1)} %get-tuple-element.49), channel_id=1, source_target_pairs={{8,0},{16,8},{24,16},{0,24},{9,1},{17,9},{25,17},{1,25},{10,2},{18... | collective-permute-start | bytes 6152 | tf_op jit(solution)/shard_map/ppermute | solution.py:35
  238.5 6.5 %collective-permute-start.48 = (f32[1,2,4,64]{3,2,1,0:T(4,128)S(1)}, f32[1,2,4,64]{3,2,1,0:T(4,128)S(1)}, u32[]{:S(2)}, u32[]{:S(2)}) collective-permute-start(f32[1,2,4,64]{3,2,1,0:T(4,128)S(1)} %get-tuple-element.45), channel_id=1, source_target_pairs={{0,8},{8,16},{16,24},{24,0},{1,9},{9,17},{17,25},{25,1},{2,10},{10... | collective-permute-start | bytes 6152 | tf_op jit(solution)/shard_map/ppermute | solution.py:33
  238.6 8.0 %collective-permute-start.49 = (f32[1,2,4,64]{3,2,1,0:T(4,128)S(1)}, f32[1,2,4,64]{3,2,1,0:T(4,128)S(1)}, u32[]{:S(2)}, u32[]{:S(2)}) collective-permute-start(f32[1,2,4,64]{3,2,1,0:T(4,128)S(1)} %get-tuple-element.45), channel_id=1, source_target_pairs={{8,0},{16,8},{24,16},{0,24},{9,1},{17,9},{25,17},{1,25},{10,2},{18... | collective-permute-start | bytes 6152 | tf_op jit(solution)/shard_map/ppermute | solution.py:35
  240.3 6.3 %collective-permute-start.46 = (f32[1,1,4,64]{3,2,1,0:T(4,128)S(1)}, f32[1,1,4,64]{3,2,1,0:T(4,128)S(1)}, u32[]{:S(2)}, u32[]{:S(2)}) collective-permute-start(f32[1,1,4,64]{3,2,1,0:T(4,128)S(1)} %get-tuple-element.47), channel_id=1, source_target_pairs={{0,1},{1,2},{2,3},{3,4},{4,5},{5,6},{6,7},{7,0},{8,9},{9,10},{10,1... | collective-permute-start | bytes 3080 | tf_op jit(solution)/shard_map/ppermute | solution.py:33
  256.4 6.3 %collective-permute-start.50 = (f32[2,4]{1,0:T(2,128)S(1)}, f32[2,4]{1,0:T(2,128)S(1)}, u32[]{:S(2)}, u32[]{:S(2)}) collective-permute-start(f32[2,4]{1,0:T(2,128)S(1)} %bitcast.266), channel_id=1, source_target_pairs={{0,1},{1,2},{2,3},{3,4},{4,5},{5,6},{6,7},{7,0},{8,9},{9,10},{10,1... | collective-permute-start | bytes 104 | tf_op jit(solution)/shard_map/ppermute | solution.py:16
  282.0 6.5 %collective-permute-start.59 = (f32[1,2,4,64]{3,2,1,0:T(4,128)S(1)}, f32[1,2,4,64]{3,2,1,0:T(4,128)S(1)}, u32[]{:S(2)}, u32[]{:S(2)}) collective-permute-start(f32[1,2,4,64]{3,2,1,0:T(4,128)S(1)} %get-tuple-element.41), channel_id=1, source_target_pairs={{0,8},{8,16},{16,24},{24,0},{1,9},{9,17},{17,25},{25,1},{2,10},{10... | collective-permute-start | bytes 6152 | tf_op jit(solution)/shard_map/ppermute | solution.py:33
  282.1 8.0 %collective-permute-start.60 = (f32[1,2,4,64]{3,2,1,0:T(4,128)S(1)}, f32[1,2,4,64]{3,2,1,0:T(4,128)S(1)}, u32[]{:S(2)}, u32[]{:S(2)}) collective-permute-start(f32[1,2,4,64]{3,2,1,0:T(4,128)S(1)} %get-tuple-element.41), channel_id=1, source_target_pairs={{8,0},{16,8},{24,16},{0,24},{9,1},{17,9},{25,17},{1,25},{10,2},{18... | collective-permute-start | bytes 6152 | tf_op jit(solution)/shard_map/ppermute | solution.py:35
  340.9 6.5 %collective-permute-start.63 = (f32[1,2,4,64]{3,2,1,0:T(4,128)S(1)}, f32[1,2,4,64]{3,2,1,0:T(4,128)S(1)}, u32[]{:S(2)}, u32[]{:S(2)}) collective-permute-start(f32[1,2,4,64]{3,2,1,0:T(4,128)S(1)} %get-tuple-element.37), channel_id=1, source_target_pairs={{0,8},{8,16},{16,24},{24,0},{1,9},{9,17},{17,25},{25,1},{2,10},{10... | collective-permute-start | bytes 6152 | tf_op jit(solution)/shard_map/ppermute | solution.py:33
  340.9 8.0 %collective-permute-start.64 = (f32[1,2,4,64]{3,2,1,0:T(4,128)S(1)}, f32[1,2,4,64]{3,2,1,0:T(4,128)S(1)}, u32[]{:S(2)}, u32[]{:S(2)}) collective-permute-start(f32[1,2,4,64]{3,2,1,0:T(4,128)S(1)} %get-tuple-element.37), channel_id=1, source_target_pairs={{8,0},{16,8},{24,16},{0,24},{9,1},{17,9},{25,17},{1,25},{10,2},{18... | collective-permute-start | bytes 6152 | tf_op jit(solution)/shard_map/ppermute | solution.py:35
  359.1 6.5 %collective-permute-start.67 = (f32[1,2,4,64]{3,2,1,0:T(4,128)S(1)}, f32[1,2,4,64]{3,2,1,0:T(4,128)S(1)}, u32[]{:S(2)}, u32[]{:S(2)}) collective-permute-start(f32[1,2,4,64]{3,2,1,0:T(4,128)S(1)} %get-tuple-element.33), channel_id=1, source_target_pairs={{0,8},{8,16},{16,24},{24,0},{1,9},{9,17},{17,25},{25,1},{2,10},{10... | collective-permute-start | bytes 6152 | tf_op jit(solution)/shard_map/ppermute | solution.py:33
  359.1 8.0 %collective-permute-start.68 = (f32[1,2,4,64]{3,2,1,0:T(4,128)S(1)}, f32[1,2,4,64]{3,2,1,0:T(4,128)S(1)}, u32[]{:S(2)}, u32[]{:S(2)}) collective-permute-start(f32[1,2,4,64]{3,2,1,0:T(4,128)S(1)} %get-tuple-element.33), channel_id=1, source_target_pairs={{8,0},{16,8},{24,16},{0,24},{9,1},{17,9},{25,17},{1,25},{10,2},{18... | collective-permute-start | bytes 6152 | tf_op jit(solution)/shard_map/ppermute | solution.py:35
  360.8 6.3 %collective-permute-start.65 = (f32[1,1,4,64]{3,2,1,0:T(4,128)S(1)}, f32[1,1,4,64]{3,2,1,0:T(4,128)S(1)}, u32[]{:S(2)}, u32[]{:S(2)}) collective-permute-start(f32[1,1,4,64]{3,2,1,0:T(4,128)S(1)} %get-tuple-element.35), channel_id=1, source_target_pairs={{0,1},{1,2},{2,3},{3,4},{4,5},{5,6},{6,7},{7,0},{8,9},{9,10},{10,1... | collective-permute-start | bytes 3080 | tf_op jit(solution)/shard_map/ppermute | solution.py:33
  376.9 6.5 %collective-permute-start.71 = (f32[1,2,4,64]{3,2,1,0:T(4,128)S(1)}, f32[1,2,4,64]{3,2,1,0:T(4,128)S(1)}, u32[]{:S(2)}, u32[]{:S(2)}) collective-permute-start(f32[1,2,4,64]{3,2,1,0:T(4,128)S(1)} %get-tuple-element.29), channel_id=1, source_target_pairs={{0,8},{8,16},{16,24},{24,0},{1,9},{9,17},{17,25},{25,1},{2,10},{10... | collective-permute-start | bytes 6152 | tf_op jit(solution)/shard_map/ppermute | solution.py:33
  376.9 8.0 %collective-permute-start.72 = (f32[1,2,4,64]{3,2,1,0:T(4,128)S(1)}, f32[1,2,4,64]{3,2,1,0:T(4,128)S(1)}, u32[]{:S(2)}, u32[]{:S(2)}) collective-permute-start(f32[1,2,4,64]{3,2,1,0:T(4,128)S(1)} %get-tuple-element.29), channel_id=1, source_target_pairs={{8,0},{16,8},{24,16},{0,24},{9,1},{17,9},{25,17},{1,25},{10,2},{18... | collective-permute-start | bytes 6152 | tf_op jit(solution)/shard_map/ppermute | solution.py:35
  394.8 6.3 %collective-permute-start.73 = (f32[2,4]{1,0:T(2,128)S(1)}, f32[2,4]{1,0:T(2,128)S(1)}, u32[]{:S(2)}, u32[]{:S(2)}) collective-permute-start(f32[2,4]{1,0:T(2,128)S(1)} %bitcast.260), channel_id=1, source_target_pairs={{0,1},{1,2},{2,3},{3,4},{4,5},{5,6},{6,7},{7,0},{8,9},{9,10},{10,1... | collective-permute-start | bytes 104 | tf_op jit(solution)/shard_map/ppermute | solution.py:16
  420.4 6.5 %collective-permute-start.82 = (f32[1,2,4,64]{3,2,1,0:T(4,128)S(1)}, f32[1,2,4,64]{3,2,1,0:T(4,128)S(1)}, u32[]{:S(2)}, u32[]{:S(2)}) collective-permute-start(f32[1,2,4,64]{3,2,1,0:T(4,128)S(1)} %get-tuple-element.25), channel_id=1, source_target_pairs={{0,8},{8,16},{16,24},{24,0},{1,9},{9,17},{17,25},{25,1},{2,10},{10... | collective-permute-start | bytes 6152 | tf_op jit(solution)/shard_map/ppermute | solution.py:33
  420.4 8.0 %collective-permute-start.83 = (f32[1,2,4,64]{3,2,1,0:T(4,128)S(1)}, f32[1,2,4,64]{3,2,1,0:T(4,128)S(1)}, u32[]{:S(2)}, u32[]{:S(2)}) collective-permute-start(f32[1,2,4,64]{3,2,1,0:T(4,128)S(1)} %get-tuple-element.25), channel_id=1, source_target_pairs={{8,0},{16,8},{24,16},{0,24},{9,1},{17,9},{25,17},{1,25},{10,2},{18... | collective-permute-start | bytes 6152 | tf_op jit(solution)/shard_map/ppermute | solution.py:35
  422.2 6.3 %collective-permute-start.80 = (f32[1,1,4,64]{3,2,1,0:T(4,128)S(1)}, f32[1,1,4,64]{3,2,1,0:T(4,128)S(1)}, u32[]{:S(2)}, u32[]{:S(2)}) collective-permute-start(f32[1,1,4,64]{3,2,1,0:T(4,128)S(1)} %get-tuple-element.27), channel_id=1, source_target_pairs={{0,1},{1,2},{2,3},{3,4},{4,5},{5,6},{6,7},{7,0},{8,9},{9,10},{10,1... | collective-permute-start | bytes 3080 | tf_op jit(solution)/shard_map/ppermute | solution.py:33
  422.2 6.3 %collective-permute-start.81 = (f32[1,1,4,64]{3,2,1,0:T(4,128)S(1)}, f32[1,1,4,64]{3,2,1,0:T(4,128)S(1)}, u32[]{:S(2)}, u32[]{:S(2)}) collective-permute-start(f32[1,1,4,64]{3,2,1,0:T(4,128)S(1)} %get-tuple-element.28), channel_id=1, source_target_pairs={{1,0},{2,1},{3,2},{4,3},{5,4},{6,5},{7,6},{0,7},{9,8},{10,9},{11,1... | collective-permute-start | bytes 3080 | tf_op jit(solution)/shard_map/ppermute | solution.py:35
  (42 other events, 278.4 us)
